TPU v7x, 32 devices: a whole 2x2x4 slice. The times are simulated.
32 devices in a mesh: horiz: 8 (over y, x, core), lev: 4 (over z).
Axes of the slice: x: 2, y: 2, z: 4, core: 2. Of those that a mesh axis runs over, the one named last changes fastest.
Arguments:
- source_state: bfloat16 [5, 68, 32768], P(None, 'lev', 'horiz'), may hold values from -6 to 6
- intersection: int32 [40], P('horiz'), may hold values from 0 to 7, as said below
- index_map: int32 [40, 512], P('horiz'), may hold values from 0 to 4095
- blocks: bfloat16 [40, 512, 2048], P('horiz'), may hold values from -0.125 to 0.125
- bracket: int32 [127, 16384], P(None, ('horiz', 'lev')), may hold values from 0 to 66
- fraction: float32 [127, 16384], P(None, ('horiz', 'lev')), may hold values from 0 to 1
Outputs:
- target_state: bfloat16 [5, 127, 16384], P(None, None, ('horiz', 'lev'))
Inputs may be any that keep to these rules, and one draw needn't show every extreme that they name: For every target group g, intersection[g * 5] to intersection[g * 5 + 4] are the groups g - 2 to g + 2 modulo 8, each once, in some order.
All inputs are finite; a program needn't handle non-finite values.
Results may differ from a plain program's by a relative error of at most 0.0049.
Values may be sent and summed in bfloat16 or wider, within the bound.
A program may use at most 64 MiB of HBM per device.

v0:
```python
import jax
import jax.numpy as jnp
from jax import lax
from jax.sharding import PartitionSpec as P


def shifted(block, axis, distance):
    devices = range(lax.axis_size(axis))
    route = [((i - distance) % len(devices), i) for i in devices]
    return lax.ppermute(block, axis, route)


def select_cells(tile, wanted):
    cell_ids = jnp.arange(tile.shape[1], dtype=jnp.int32)[:, None]
    picker = (cell_ids == wanted[None, :]).astype(jnp.bfloat16)
    return jnp.dot(tile, picker, preferred_element_type=jnp.float32).astype(jnp.bfloat16)


def local(source_state, intersection, index_map, blocks, bracket, fraction):
    fields, level_slab, tile_cells = source_state.shape
    stacked = source_state.reshape(fields * level_slab, tile_cells)
    groups = lax.axis_size("horiz")
    block_count = intersection.shape[0]
    depth = (block_count - 1) // 2
    own_group = lax.axis_index("horiz")
    position = (intersection - own_group + depth) % groups
    collected = []
    for offset in range(-depth, depth + 1):
        wanted_group = (own_group + offset) % groups
        matched = intersection == wanted_group
        request = jnp.sum(jnp.where(matched[:, None], index_map, 0), axis=0)
        if offset == 0:
            collected.append(select_cells(stacked, request))
        else:
            incoming = shifted(request, "horiz", offset)
            outgoing = select_cells(stacked, incoming)
            collected.append(shifted(outgoing, "horiz", -offset))
    by_offset = jnp.stack(collected)
    pieces = [
        lax.dynamic_index_in_dim(by_offset, position[block_slot], 0, keepdims=False)
        for block_slot in range(block_count)
    ]
    chosen = jnp.concatenate(pieces, axis=1)
    weights_flat = blocks.reshape(-1, blocks.shape[2])
    horizontal = jnp.dot(chosen, weights_flat, preferred_element_type=jnp.float32).astype(
        jnp.bfloat16
    )
    horizontal = horizontal.reshape(fields, level_slab, blocks.shape[2])
    level_total = level_slab * lax.axis_size("lev")
    level_ids = jnp.arange(level_total, dtype=jnp.int32)[None, :, None]
    lower_hit = level_ids == bracket[:, None, :]
    upper_hit = level_ids == bracket[:, None, :] + 1
    upper_share = fraction[:, None, :]
    interp = jnp.where(lower_hit, 1.0 - upper_share, 0.0) + jnp.where(upper_hit, upper_share, 0.0)
    widened = lax.all_to_all(horizontal, "lev", split_axis=2, concat_axis=1, tiled=True).astype(
        jnp.float32
    )
    mixed = jnp.einsum("jlc,flc->fjc", interp, widened, precision=lax.Precision.HIGHEST)
    return mixed.astype(jnp.bfloat16)


def solution(mesh):
    in_specs = (
        P(None, "lev", "horiz"),
        P("horiz"),
        P("horiz", None),
        P("horiz", None, None),
        P(None, ("horiz", "lev")),
        P(None, ("horiz", "lev")),
    )
    out_specs = P(None, None, ("horiz", "lev"))
    return jax.shard_map(local, mesh=mesh, in_specs=in_specs, out_specs=out_specs, check_vma=False)
```

profile of v0, /device:TPU:0, one launch (start us, length us, event | category | flops | bytes accessed | tf_op | source)
XLA Modules:
  0.0 83.7 jit_solution(5691113030933345913)
XLA Ops:
  0.0 0.7 broadcast_compare_fusion.1
  0.7 0.8 select_reduce_fusion
  1.5 3.4 %collective-permute-start.2 = (s32[512]{0:T(512)S(1)}, s32[512]{0:T(512)S(1)}, u32[]{:S(2)}, u32[]{:S(2)}) collective-permute-start(s32[512]{0:T(512)S(1)} %get-tuple-element.7), channel_id=1, source_target_pairs={{4,0},{8,4},{12,8},{16,12},{20,16},{24,20},{28,24},{0,28},{5,1},{9... | collective-permute-start | bytes 6152 | tf_op jit(solution)/shard_map/ppermute | solution.py:10
  4.9 0.6 collective-permute-start
  5.5 0.2 collective-permute-start.4
  5.7 1.2 %collective-permute-start.6 = (s32[512]{0:T(512)S(1)}, s32[512]{0:T(512)S(1)}, u32[]{:S(2)}, u32[]{:S(2)}) collective-permute-start(s32[512]{0:T(512)S(1)} %get-tuple-element.5), channel_id=1, source_target_pairs={{24,0},{28,4},{0,8},{4,12},{8,16},{12,20},{16,24},{20,28},{25,1},{... | collective-permute-start | bytes 6152 | tf_op jit(solution)/shard_map/ppermute | solution.py:10
  6.9 0.7 and_select_fusion
  7.6 0.7 fusion.38
  14.7 1.4 %reshape.25 = bf16[85,4096]{1,0:T(8,128)(2,1)S(1)} reshape(bf16[5,17,4096]{2,1,0:T(8,128)(2,1)} %param.6) | data formatting | bytes 1392640 | tf_op jit(solution)/shard_map/reshape | solution.py:21
  19.4 1.5 %fusion.31 = bf16[85,512]{1,0:T(8,128)(2,1)S(1)} fusion(bf16[85,4096]{1,0:T(8,128)(2,1)S(1)} %reshape.25, s32[512]{0:T(512)S(1)} %collective-permute-done.2), kind=kOutput, calls=%fused_computation.35 | convolution fusion | flops 358656512 | bytes 785408 | tf_op jit(solution)/shard_map/dot_general | solution.py:16
  20.9 0.5 collective-permute-start.3
  21.3 1.5 %fusion.30 = bf16[85,512]{1,0:T(8,128)(2,1)S(1)} fusion(bf16[85,4096]{1,0:T(8,128)(2,1)S(1)} %reshape.25, s32[512]{0:T(512)S(1)} %collective-permute-done), kind=kOutput, calls=%fused_computation.34 | convolution fusion | flops 358656512 | bytes 785408 | tf_op jit(solution)/shard_map/dot_general | solution.py:16
  22.8 1.4 %collective-permute-start.1 = (bf16[85,512]{1,0:T(8,128)(2,1)S(1)}, bf16[85,512]{1,0:T(8,128)(2,1)S(1)}, u32[]{:S(2)}, u32[]{:S(2)}) collective-permute-start(bf16[85,512]{1,0:T(8,128)(2,1)S(1)} %fusion.30), channel_id=1, source_target_pairs={{24,0},{28,4},{0,8},{4,12},{8,16},{12,20},{16,24},{20,28},{25,1},{... | collective-permute-start | bytes 261128 | tf_op jit(solution)/shard_map/ppermute | solution.py:10
  24.2 1.5 %fusion.34 = bf16[85,512]{1,0:T(8,128)(2,1)S(1)} fusion(bf16[85,4096]{1,0:T(8,128)(2,1)S(1)} %reshape.25, s32[512]{0:T(512)S(1)} %collective-permute-done.4), kind=kOutput, calls=%fused_computation.38 | convolution fusion | flops 358656512 | bytes 785408 | tf_op jit(solution)/shard_map/dot_general | solution.py:16
  25.7 1.3 %collective-permute-start.5 = (bf16[85,512]{1,0:T(8,128)(2,1)S(1)}, bf16[85,512]{1,0:T(8,128)(2,1)S(1)}, u32[]{:S(2)}, u32[]{:S(2)}) collective-permute-start(bf16[85,512]{1,0:T(8,128)(2,1)S(1)} %fusion.34), channel_id=1, source_target_pairs={{4,0},{8,4},{12,8},{16,12},{20,16},{24,20},{28,24},{0,28},{5,1},{9... | collective-permute-start | bytes 261128 | tf_op jit(solution)/shard_map/ppermute | solution.py:10
  27.1 1.5 %fusion.35 = bf16[85,512]{1,0:T(8,128)(2,1)S(1)} fusion(bf16[85,4096]{1,0:T(8,128)(2,1)S(1)} %reshape.25, s32[512]{0:T(512)S(1)} %collective-permute-done.6), kind=kOutput, calls=%fused_computation.39 | convolution fusion | flops 358656512 | bytes 785408 | tf_op jit(solution)/shard_map/dot_general | solution.py:16
  28.6 1.3 %collective-permute-start.7 = (bf16[85,512]{1,0:T(8,128)(2,1)S(1)}, bf16[85,512]{1,0:T(8,128)(2,1)S(1)}, u32[]{:S(2)}, u32[]{:S(2)}) collective-permute-start(bf16[85,512]{1,0:T(8,128)(2,1)S(1)} %fusion.35), channel_id=1, source_target_pairs={{8,0},{12,4},{16,8},{20,12},{24,16},{28,20},{0,24},{4,28},{9,1},{1... | collective-permute-start | bytes 261128 | tf_op jit(solution)/shard_map/ppermute | solution.py:10
  29.9 1.5 %fusion.33 = bf16[5,85,512]{2,1,0:T(8,128)(2,1)S(1)} fusion(bf16[5,85,512]{2,1,0:T(8,128)(2,1)S(1)} %bitcast_dynamic-update-slice_fusion.7, bf16[85,4096]{1,0:T(8,128)(2,1)S(1)} %reshape.25, s32[512]{0:T(512)S(1)} %get-tuple-element.6), kind=kOutput, calls=%fused_computation.37 | convolution fusion | flops 358656512 | bytes 813056 | tf_op jit(solution)/shard_map/dot_general | solution.py:16
  31.5 1.7 %collective-permute-done.7 = bf16[85,512]{1,0:T(8,128)(2,1)S(1)} collective-permute-done((bf16[85,512]{1,0:T(8,128)(2,1)S(1)}, bf16[85,512]{1,0:T(8,128)(2,1)S(1)}, u32[]{:S(2)}, u32[]{:S(2)}) %collective-permute-start.7) | collective-permute-done | bytes 87072 | tf_op jit(solution)/shard_map/ppermute | solution.py:10
  33.3 1.9 %convolution_convert_fusion = bf16[85,2048]{1,0:T(8,128)(2,1)S(1)} fusion(bf16[85,2560]{1,0:T(8,128)(2,1)S(1)} %bitcast_dynamic-update-slice_fusion, bf16[2560,2048]{1,0:T(8,128)(2,1)S(1)} %bitcast.54), kind=kOutput, calls=%fused_computation.26 | convolution fusion | flops 891463680 | bytes 11269120 | tf_op jit(solution)/shard_map/dot_general | solution.py:45
  35.3 4.2 %copy.26 = bf16[5,17,2048]{1,0,2:T(8,128)(2,1)} copy(bf16[5,17,2048]{2,1,0:T(8,128)(2,1)S(1)} %reshape.27) | data formatting | bytes 696320 | tf_op jit(solution)/shard_map/reshape | solution.py:48
  39.5 5.9 %reshape.28 = bf16[4,2,21760]{2,1,0:T(2,128)(2,1)} reshape(bf16[2048,5,17]{2,1,0:T(8,128)(2,1)} %bitcast.55) | data formatting | bytes 696320
  45.4 4.9 %all-to-all-start = ((bf16[4,2,21760]{2,1,0:T(2,128)(2,1)}), bf16[4,2,21760]{2,1,0:T(2,128)(2,1)S(1)}, u32[]{:S(2)}, u32[]{:S(2)}) async-start(bf16[4,2,21760]{2,1,0:T(2,128)(2,1)} %reshape.28), calls=%async_computation | async-start | bytes 696320 | tf_op jit(solution)/shard_map/all_to_all | solution.py:55
  50.5 0.1 copy.30
  50.6 0.1 copy.29
  50.8 0.1 copy.31
  50.9 8.3 %all-to-all-done = bf16[4,2,21760]{2,1,0:T(2,128)(2,1)S(1)} async-done(((bf16[4,2,21760]{2,1,0:T(2,128)(2,1)}), bf16[4,2,21760]{2,1,0:T(2,128)(2,1)S(1)}, u32[]{:S(2)}, u32[]{:S(2)}) %all-to-all-start) | async-done | bytes 348192 | tf_op jit(solution)/shard_map/all_to_all | solution.py:55
  59.3 5.0 %reshape.29 = bf16[2048,5,17]{2,1,0:T(8,128)(2,1)} reshape(bf16[4,2,21760]{2,1,0:T(2,128)(2,1)S(1)} %all-to-all-done) | data formatting | bytes 696320
  64.2 4.2 %copy.35 = bf16[5,17,4,512]{3,2,1,0:T(4,128)(2,1)S(1)} copy(bf16[5,17,4,512]{1,0,3,2:T(8,128)(2,1)} %bitcast.56) | data formatting | bytes 696320 | tf_op jit(solution)/shard_map/all_to_all | solution.py:55
  68.7 0.8 copy.33
  69.4 12.9 %fusion.22 = bf16[5,127,512]{1,0,2:T(8,128)(2,1)S(1)} fusion(bf16[5,68,512]{1,0,2:T(8,128)(2,1)S(1)} %copy.33, f32[127,512]{0,1:T(8,128)S(1)} %copy.32, s32[127,512]{0,1:T(8,128)S(1)} %copy.31, f32[127,512]{0,1:T(8,128)S(1)} %copy.30, s32[127,512]{0,1:T(8,128)S(1)} %copy.29), kind=kOutput, calls=%fused_computation.28 | convolution fusion | flops 287731200 | bytes 2038784 | tf_op jit(solution)/shard_map/jlc,flc->fjc/dot_general | solution.py:58
  82.4 1.4 %copy.34 = bf16[5,127,512]{2,1,0:T(8,128)(2,1)} copy(bf16[5,127,512]{1,0,2:T(8,128)(2,1)S(1)} %fusion.22) | data formatting | bytes 1300480 | tf_op jit(solution)/shard_map/convert_element_type | solution.py:59
  (33 shorter events, 0.6 us)
Async XLA Ops:
  1.5 17.9 %collective-permute-start.2 = (s32[512]{0:T(512)S(1)}, s32[512]{0:T(512)S(1)}, u32[]{:S(2)}, u32[]{:S(2)}) collective-permute-start(s32[512]{0:T(512)S(1)} %get-tuple-element.7), channel_id=1, source_target_pairs={{4,0},{8,4},{12,8},{16,12},{20,16},{24,20},{28,24},{0,28},{5,1},{9... | collective-permute-start | bytes 6152 | tf_op jit(solution)/shard_map/ppermute | solution.py:10
  4.9 16.4 %collective-permute-start = (s32[512]{0:T(512)S(1)}, s32[512]{0:T(512)S(1)}, u32[]{:S(2)}, u32[]{:S(2)}) collective-permute-start(s32[512]{0:T(512)S(1)} %get-tuple-element.8), channel_id=1, source_target_pairs={{8,0},{12,4},{16,8},{20,12},{24,16},{28,20},{0,24},{4,28},{9,1},{1... | collective-permute-start | bytes 6152 | tf_op jit(solution)/shard_map/ppermute | solution.py:10
  5.5 18.7 %collective-permute-start.4 = (s32[512]{0:T(512)S(1)}, s32[512]{0:T(512)S(1)}, u32[]{:S(2)}, u32[]{:S(2)}) collective-permute-start(s32[512]{0:T(512)S(1)} %get-tuple-element.9), channel_id=1, source_target_pairs={{28,0},{0,4},{4,8},{8,12},{12,16},{16,20},{20,24},{24,28},{29,1},{... | collective-permute-start | bytes 6152 | tf_op jit(solution)/shard_map/ppermute | solution.py:10
  5.7 21.4 %collective-permute-start.6 = (s32[512]{0:T(512)S(1)}, s32[512]{0:T(512)S(1)}, u32[]{:S(2)}, u32[]{:S(2)}) collective-permute-start(s32[512]{0:T(512)S(1)} %get-tuple-element.5), channel_id=1, source_target_pairs={{24,0},{28,4},{0,8},{4,12},{8,16},{12,20},{16,24},{20,28},{25,1},{... | collective-permute-start | bytes 6152 | tf_op jit(solution)/shard_map/ppermute | solution.py:10
  19.3 13.9 %slice-start = ((s8[10485760]{0:T(1024)(128)(4,1)}), s8[4194304]{0:T(1024)(128)(4,1)S(1)}, s32[]{:S(2)}) async-start(s8[10485760]{0:T(1024)(128)(4,1)} %bitcast.52), calls=%async_computation.1 | async-start | bytes 8388608
  20.8 12.4 %slice-start.1 = ((s8[10485760]{0:T(1024)(128)(4,1)}), s8[4194304]{0:T(1024)(128)(4,1)S(1)}, s32[]{:S(2)}) async-start(s8[10485760]{0:T(1024)(128)(4,1)} %bitcast.52), calls=%async_computation.2 | async-start | bytes 8388608
  20.9 9.1 %collective-permute-start.3 = (bf16[85,512]{1,0:T(8,128)(2,1)S(1)}, bf16[85,512]{1,0:T(8,128)(2,1)S(1)}, u32[]{:S(2)}, u32[]{:S(2)}) collective-permute-start(bf16[85,512]{1,0:T(8,128)(2,1)S(1)} %fusion.31), channel_id=1, source_target_pairs={{28,0},{0,4},{4,8},{8,12},{12,16},{16,20},{20,24},{24,28},{29,1},{... | collective-permute-start | bytes 261128 | tf_op jit(solution)/shard_map/ppermute | solution.py:10
  22.8 7.1 %collective-permute-start.1 = (bf16[85,512]{1,0:T(8,128)(2,1)S(1)}, bf16[85,512]{1,0:T(8,128)(2,1)S(1)}, u32[]{:S(2)}, u32[]{:S(2)}) collective-permute-start(bf16[85,512]{1,0:T(8,128)(2,1)S(1)} %fusion.30), channel_id=1, source_target_pairs={{24,0},{28,4},{0,8},{4,12},{8,16},{12,20},{16,24},{20,28},{25,1},{... | collective-permute-start | bytes 261128 | tf_op jit(solution)/shard_map/ppermute | solution.py:10
  25.7 7.6 %slice-start.2 = ((s8[10485760]{0:T(1024)(128)(4,1)}), s8[2097152]{0:T(1024)(128)(4,1)S(1)}, s32[]{:S(2)}) async-start(s8[10485760]{0:T(1024)(128)(4,1)} %bitcast.52), calls=%async_computation.3 | async-start | bytes 4194304
  25.7 5.7 %collective-permute-start.5 = (bf16[85,512]{1,0:T(8,128)(2,1)S(1)}, bf16[85,512]{1,0:T(8,128)(2,1)S(1)}, u32[]{:S(2)}, u32[]{:S(2)}) collective-permute-start(bf16[85,512]{1,0:T(8,128)(2,1)S(1)} %fusion.34), channel_id=1, source_target_pairs={{4,0},{8,4},{12,8},{16,12},{20,16},{24,20},{28,24},{0,28},{5,1},{9... | collective-permute-start | bytes 261128 | tf_op jit(solution)/shard_map/ppermute | solution.py:10
  28.6 4.6 %collective-permute-start.7 = (bf16[85,512]{1,0:T(8,128)(2,1)S(1)}, bf16[85,512]{1,0:T(8,128)(2,1)S(1)}, u32[]{:S(2)}, u32[]{:S(2)}) collective-permute-start(bf16[85,512]{1,0:T(8,128)(2,1)S(1)} %fusion.35), channel_id=1, source_target_pairs={{8,0},{12,4},{16,8},{20,12},{24,16},{28,20},{0,24},{4,28},{9,1},{1... | collective-permute-start | bytes 261128 | tf_op jit(solution)/shard_map/ppermute | solution.py:10
  35.2 15.1 %copy-start = (f32[127,512]{1,0:T(8,128)S(1)}, f32[127,512]{1,0:T(8,128)}, u32[]{:S(2)}) copy-start(f32[127,512]{1,0:T(8,128)} %param.11) | copy-start | bytes 780292
  35.2 15.4 %copy-start.1 = (s32[127,512]{1,0:T(8,128)S(1)}, s32[127,512]{1,0:T(8,128)}, u32[]{:S(2)}) copy-start(s32[127,512]{1,0:T(8,128)} %param.10) | copy-start | bytes 780292
  45.4 13.8 %all-to-all-start = ((bf16[4,2,21760]{2,1,0:T(2,128)(2,1)}), bf16[4,2,21760]{2,1,0:T(2,128)(2,1)S(1)}, u32[]{:S(2)}, u32[]{:S(2)}) async-start(bf16[4,2,21760]{2,1,0:T(2,128)(2,1)} %reshape.28), calls=%async_computation | async-start | bytes 696320 | tf_op jit(solution)/shard_map/all_to_all | solution.py:55
where the time goes:
time: 84.6 us; the launch traced here: 83.7 us
  local copies, waits for them, and re-layouts  24.5 us (29%)
  matrix products  22.2 us (26%)
  starting transfers between devices  14.9 us (18%)
  waiting for transfers between devices  10 us (12%)
  between operations  9.9 us (12%)
  other arithmetic  2.19 us (3%)
    dot_general x1, matrix products, local(): jnp.einsum('jlc,flc->fjc', interp, widened, precision=lax.Precision.HIGHEST)  12.9 us
    unnamed x21, local copies, waits for them, and re-layouts  11.2 us
    ppermute x8, starting transfers between devices, shifted(): return lax.ppermute(block, axis, route)  10 us
    all_to_all x1, waiting for transfers between devices, local(): lax.all_to_all(horizontal, 'lev', split_axis=2, concat_axis=1, tiled=True)  8.33 us
    dot_general x5, matrix products, select_cells(): jnp.dot(tile, picker, preferred_element_type=jnp.float32)  7.4 us
    all_to_all x4, local copies, waits for them, and re-layouts, local(): lax.all_to_all(horizontal, 'lev', split_axis=2, concat_axis=1, tiled=True)  5.19 us
    all_to_all x1, starting transfers between devices, local(): lax.all_to_all(horizontal, 'lev', split_axis=2, concat_axis=1, tiled=True)  4.87 us
    reshape x2, local copies, waits for them, and re-layouts, local(): horizontal = horizontal.reshape(fields, level_slab, blocks.shape[2])  4.33 us
  transfers between devices with their start and end apart: 9, of which 2 were waited for; matrix products, arithmetic and copies ran while one was open for 13% of the time, Pallas kernels for 0%

commit v1 on v0

v1 whole, which is shorter than its diff:
```python
import functools

import jax
import jax.numpy as jnp
from jax import lax
from jax.experimental import pallas as pl
from jax.experimental.pallas import tpu as pltpu
from jax.sharding import PartitionSpec as P

MESH = pl.DeviceIdType.MESH
HIGH = 256


def round_up(value, step):
    return (value + step - 1) // step * step


def remap_kernel(
    groups, levs, depth,
    inter_ref, index_ref, source_hbm, blocks_hbm, out_ref,
    tile, stack32, stack, weights, request, wanted, chosen, arrived, total, slab,
    tile_sem, weight_sem, req_send, req_recv, val_send, val_recv, lev_send, lev_recv,
):
    fields, slab_levels, cells = tile.shape
    rows = stack.shape[0]
    count = 2 * depth + 1
    me = lax.axis_index("horiz")
    my_lev = lax.axis_index("lev")
    columns = out_ref.shape[2]

    barrier = pltpu.get_barrier_semaphore()
    offsets = [o for o in range(-depth, depth + 1) if o != 0]
    for offset in offsets:
        pl.semaphore_signal(
            barrier, inc=1, device_id={"horiz": lax.rem(me + offset + groups, groups)}, device_id_type=MESH
        )
    for hop in range(1, levs):
        pl.semaphore_signal(
            barrier, inc=1, device_id={"lev": lax.rem(my_lev + hop, levs)}, device_id_type=MESH
        )

    tile_copy = pltpu.make_async_copy(source_hbm, tile, tile_sem)
    tile_copy.start()
    weight_copies = []
    for part in range(levs):
        copy = pltpu.make_async_copy(
            blocks_hbm.at[:, :, pl.ds(part * columns, columns)], weights.at[:, part], weight_sem.at[part]
        )
        copy.start()
        weight_copies.append(copy)

    slots = []
    for place in range(count):
        group = lax.rem(me + place - depth + groups, groups)
        cells_wanted = jnp.zeros((1, index_ref.shape[1]), jnp.int32)
        slot = jnp.int32(0)
        for k in range(count):
            hit = (inter_ref[k] == group).astype(jnp.int32)
            cells_wanted = cells_wanted + index_ref[k : k + 1, :] * hit
            slot = jnp.where(inter_ref[k] == group, jnp.int32(k), slot)
        slots.append(slot)
        if place == depth:
            wanted[place] = cells_wanted
        else:
            request[place] = cells_wanted

    tile_copy.wait()
    for field in range(fields):
        stack32[pl.ds(field * slab_levels, slab_levels), :] = tile[field].astype(jnp.float32)
    spare = rows - fields * slab_levels
    if spare:
        stack32[pl.ds(fields * slab_levels, spare), :] = jnp.zeros((spare, cells), jnp.float32)
    stack[...] = stack32[...].astype(jnp.bfloat16)

    pl.semaphore_wait(barrier, len(offsets) + levs - 1)

    def request_copy(place):
        return pltpu.make_async_remote_copy(
            src_ref=request.at[place],
            dst_ref=wanted.at[2 * depth - place],
            send_sem=req_send.at[place],
            recv_sem=req_recv.at[2 * depth - place],
            device_id={"horiz": lax.rem(me + place - depth + groups, groups)},
            device_id_type=MESH,
        )

    def value_copy(place):
        return pltpu.make_async_remote_copy(
            src_ref=chosen.at[place],
            dst_ref=arrived.at[2 * depth - place],
            send_sem=val_send.at[place],
            recv_sem=val_recv.at[2 * depth - place],
            device_id={"horiz": lax.rem(me + place - depth + groups, groups)},
            device_id_type=MESH,
        )

    for reach in range(depth, 0, -1):
        request_copy(depth - reach).start()
        request_copy(depth + reach).start()

    ids = lax.broadcasted_iota(jnp.int32, (HIGH, 1), 0).astype(jnp.float32).astype(jnp.bfloat16)

    def select(place):
        cell = wanted[place]
        high = cell // HIGH
        low = (cell - high * HIGH).astype(jnp.float32)
        values = jnp.zeros((rows, cell.shape[1]), jnp.float32)
        for chunk in range(cells // HIGH):
            here = jnp.where(high == chunk, low, -1.0).astype(jnp.bfloat16)
            picker = jnp.where(ids == here, jnp.bfloat16(1), jnp.bfloat16(0))
            values += jnp.dot(
                stack[:, chunk * HIGH : (chunk + 1) * HIGH], picker, preferred_element_type=jnp.float32
            )
        return values.astype(jnp.bfloat16)

    arrived[depth] = select(depth)

    def serve(step, carry):
        reach = depth - step // 2
        place = depth + reach * (1 - 2 * (step % 2))
        request_copy(2 * depth - place).wait_recv()
        chosen[place] = select(place)
        value_copy(place).start()
        return carry

    lax.fori_loop(0, 2 * depth, serve, 0)

    for copy in weight_copies:
        copy.wait()
    order = [depth]
    for reach in range(depth, 0, -1):
        order += [depth - reach, depth + reach]
    for number, place in enumerate(order):
        if number:
            value_copy(2 * depth - place).wait_recv()
        values = arrived[place]
        for hop in list(range(1, levs)) + [0]:
            part = lax.rem(my_lev + hop, levs)
            term = jnp.dot(values, weights[slots[place], part], preferred_element_type=jnp.float32)
            if number == 0:
                total[part] = term
            elif number < count - 1:
                total[part] += term
            else:
                done = (total[part] + term).astype(jnp.bfloat16)
                if hop == 0:
                    out_ref[my_lev] = done
                else:
                    slab[hop] = done
                    lev_copy(hop, part, my_lev, slab, out_ref, lev_send, lev_recv).start()
    for hop in range(1, levs):
        lev_copy(hop, lax.rem(my_lev + hop, levs), my_lev, slab, out_ref, lev_send, lev_recv).wait()
    for offset in offsets:
        request_copy(depth + offset).wait_send()
        value_copy(depth + offset).wait_send()


def lev_copy(hop, part, my_lev, slab, out_ref, lev_send, lev_recv):
    return pltpu.make_async_remote_copy(
        src_ref=slab.at[hop],
        dst_ref=out_ref.at[my_lev],
        send_sem=lev_send.at[hop],
        recv_sem=lev_recv.at[hop],
        device_id={"lev": part},
        device_id_type=MESH,
    )


def rows_at(table, index):
    numbers = lax.GatherDimensionNumbers(
        offset_dims=(),
        collapsed_slice_dims=(0,),
        start_index_map=(0,),
        operand_batching_dims=(1,),
        start_indices_batching_dims=(1,),
    )
    return lax.gather(
        table, index[..., None], numbers, slice_sizes=(1, 1), mode=lax.GatherScatterMode.PROMISE_IN_BOUNDS
    )


def levels_kernel(slab_levels, slabs_ref, bracket_ref, fraction_ref, out_ref, raw, table):
    levs = slabs_ref.shape[0]
    fields, levels_out, lanes = out_ref.shape
    total = levs * slab_levels
    raw[...] = slabs_ref[...].astype(jnp.float32)
    for field in range(fields):
        for lev in range(levs):
            table[field, pl.ds(lev * slab_levels, slab_levels), :] = raw[
                lev, pl.ds(field * slab_levels, slab_levels), :
            ]
        table[field, pl.ds(total, table.shape[1] - total), :] = jnp.zeros(
            (table.shape[1] - total, lanes), jnp.float32
        )
    step = 16
    for start in range(0, levels_out, step):
        size = min(step, levels_out - start)
        bracket = bracket_ref[start : start + size, :]
        upper = fraction_ref[start : start + size, :]
        if size < step:
            bracket = jnp.concatenate([bracket, jnp.zeros((step - size, lanes), jnp.int32)], axis=0)
            upper = jnp.concatenate([upper, jnp.zeros((step - size, lanes), jnp.float32)], axis=0)
        halves = [bracket[i : i + 8] for i in range(0, step, 8)]
        high = [half >> 3 for half in halves]
        low = [half & 7 for half in halves]
        below = [[jnp.zeros((8, lanes), jnp.float32) for _ in halves] for _ in range(fields)]
        above = [[jnp.zeros((8, lanes), jnp.float32) for _ in halves] for _ in range(fields)]
        for group in range((total - 2) // 8 + 1):
            masks = [h == group for h in high]
            for field in range(fields):
                here = table[field, pl.ds(group * 8, 8), :]
                over = table[field, pl.ds(group * 8 + 1, 8), :]
                for i, mask in enumerate(masks):
                    below[field][i] = jnp.where(mask, rows_at(here, low[i]), below[field][i])
                    above[field][i] = jnp.where(mask, rows_at(over, low[i]), above[field][i])
        for field in range(fields):
            mixed = (1.0 - upper) * jnp.concatenate(below[field], axis=0) + upper * jnp.concatenate(
                above[field], axis=0
            )
            out_ref[field, start : start + size, :] = mixed[:size].astype(jnp.bfloat16)


def local(levs, groups, source_state, intersection, index_map, blocks, bracket, fraction):
    fields, slab_levels, cells = source_state.shape
    count, wide, targets = blocks.shape
    depth = (count - 1) // 2
    rows = round_up(fields * slab_levels, 8)
    columns = targets // levs
    slabs = pl.pallas_call(
        functools.partial(remap_kernel, groups, levs, depth),
        name="remap",
        out_shape=jax.ShapeDtypeStruct((levs, rows, columns), jnp.bfloat16),
        in_specs=[
            pl.BlockSpec(memory_space=pltpu.SMEM),
            pl.BlockSpec(memory_space=pltpu.VMEM),
            pl.BlockSpec(memory_space=pl.ANY),
            pl.BlockSpec(memory_space=pl.ANY),
        ],
        out_specs=pl.BlockSpec(memory_space=pltpu.VMEM),
        scratch_shapes=[
            pltpu.VMEM((fields, slab_levels, cells), jnp.bfloat16),
            pltpu.VMEM((rows, cells), jnp.float32),
            pltpu.VMEM((rows, cells), jnp.bfloat16),
            pltpu.VMEM((count, levs, wide, columns), jnp.bfloat16),
            pltpu.VMEM((count, 1, wide), jnp.int32),
            pltpu.VMEM((count, 1, wide), jnp.int32),
            pltpu.VMEM((count, rows, wide), jnp.bfloat16),
            pltpu.VMEM((count, rows, wide), jnp.bfloat16),
            pltpu.VMEM((levs, rows, columns), jnp.float32),
            pltpu.VMEM((levs, rows, columns), jnp.bfloat16),
            pltpu.SemaphoreType.DMA,
            pltpu.SemaphoreType.DMA((levs,)),
            pltpu.SemaphoreType.DMA((count,)),
            pltpu.SemaphoreType.DMA((count,)),
            pltpu.SemaphoreType.DMA((count,)),
            pltpu.SemaphoreType.DMA((count,)),
            pltpu.SemaphoreType.DMA((levs,)),
            pltpu.SemaphoreType.DMA((levs,)),
        ],
        compiler_params=pltpu.CompilerParams(
            collective_id=0, has_side_effects=True, vmem_limit_bytes=48 * 1024 * 1024
        ),
    )(intersection, index_map, source_state, blocks)
    levels_out, held = bracket.shape
    lanes = 128
    return pl.pallas_call(
        functools.partial(levels_kernel, slab_levels),
        name="levels",
        grid=(held // lanes,),
        out_shape=jax.ShapeDtypeStruct((fields, levels_out, held), jnp.bfloat16),
        in_specs=[
            pl.BlockSpec((levs, rows, lanes), lambda i: (0, 0, i)),
            pl.BlockSpec((levels_out, lanes), lambda i: (0, i)),
            pl.BlockSpec((levels_out, lanes), lambda i: (0, i)),
        ],
        out_specs=pl.BlockSpec((fields, levels_out, lanes), lambda i: (0, 0, i)),
        scratch_shapes=[
            pltpu.VMEM((levs, rows, lanes), jnp.float32),
            pltpu.VMEM((fields, round_up(levs * slab_levels, 8) + 8, lanes), jnp.float32),
        ],
    )(slabs, bracket, fraction)


def solution(mesh):
    in_specs = (
        P(None, "lev", "horiz"),
        P("horiz"),
        P("horiz", None),
        P("horiz", None, None),
        P(None, ("horiz", "lev")),
        P(None, ("horiz", "lev")),
    )
    out_specs = P(None, None, ("horiz", "lev"))
    body = functools.partial(local, mesh.shape["lev"], mesh.shape["horiz"])
    return jax.shard_map(body, mesh=mesh, in_specs=in_specs, out_specs=out_specs, check_vma=False)
```

time: 84.6 us -> 33.3 us (0.39)
  Pallas kernels: 0 us -> 29.7 us
  matrix products: 22.2 us -> 0 us
  local copies, waits for them, and re-layouts: 24.5 us -> 3.3 us
  starting transfers between devices: 14.9 us -> 0 us
  waiting for transfers between devices: 10 us -> 0 us
  between operations: 9.9 us -> 0.02 us
  other arithmetic: 2.19 us -> 0 us
    pallas_call x0 -> x2, Pallas kernels: none -> 29.7 us  [the longest x1 25.5 us: local(): pl.pallas_call(functools.partial(remap_kernel, groups, levs, depth), name...]
    dot_general x7 -> x0, matrix products: 22.2 us -> none  [the longest x1 12.9 us: local(): jnp.einsum('jlc,flc->fjc', interp, widened, precision=lax.Precision.HIGHEST)]
    ppermute x8 -> x0, starting transfers between devices: 10 us -> none  [shifted(): return lax.ppermute(block, axis, route)]
    all_to_all x1 -> x0, waiting for transfers between devices: 8.33 us -> none  [local(): lax.all_to_all(horizontal, 'lev', split_axis=2, concat_axis=1, tiled=True)]
    unnamed x21 -> x8, local copies, waits for them, and re-layouts: 11.2 us -> 3.3 us
    reshape x3 -> x0, local copies, waits for them, and re-layouts: 5.77 us -> none  [the longest x2 4.33 us: local(): horizontal = horizontal.reshape(fields, level_slab, blocks.shape[2])]
    all_to_all x4 -> x0, local copies, waits for them, and re-layouts: 5.19 us -> none  [local(): lax.all_to_all(horizontal, 'lev', split_axis=2, concat_axis=1, tiled=True)]
    all_to_all x1 -> x0, starting transfers between devices: 4.87 us -> none  [local(): lax.all_to_all(horizontal, 'lev', split_axis=2, concat_axis=1, tiled=True)]
  transfers between devices with their start and end apart: 9 -> 0, of which waited for: 2 -> 0; matrix products, arithmetic and copies ran while one was open for 13% -> 0% of each run, Pallas kernels for 0% -> 0%
where the time goes in v1:
time: 33.3 us; the launch traced here: 33 us
  Pallas kernels  29.7 us (89%)
  local copies, waits for them, and re-layouts  3.3 us (10%)
    pallas_call x1, Pallas kernels, local(): pl.pallas_call(functools.partial(remap_kernel, groups, levs, depth), name...  25.5 us
    pallas_call x1, Pallas kernels, local(): pl.pallas_call(functools.partial(levels_kernel, slab_levels), name='level...  4.16 us
    unnamed x8, local copies, waits for them, and re-layouts  3.3 us

profile of v1, /device:TPU:0, one launch (start us, length us, event | category | flops | bytes accessed | tf_op | source)
XLA Modules:
  0.0 33.0 jit_solution(16108912196860360459)
XLA Ops:
  0.0 0.0 copy-start.1
  0.0 1.2 %copy-done.1 = bf16[5,17,4096]{2,1,0:T(8,128)(2,1)S(1)} copy-done((bf16[5,17,4096]{2,1,0:T(8,128)(2,1)S(1)}, bf16[5,17,4096]{2,1,0:T(8,128)(2,1)}, u32[]{:S(2)}) %copy-start.1) | copy-done | bytes 696344
  1.2 0.0 copy-start.2
  1.2 0.7 %copy-done.2 = s32[5,512]{1,0:T(8,128)S(1)} copy-done((s32[5,512]{1,0:T(8,128)S(1)}, s32[5,512]{1,0:T(8,128)}, u32[]{:S(2)}) %copy-start.2) | copy-done | bytes 10264
  1.9 0.0 copy-start.3
  1.9 0.7 %copy-done.3 = s32[5]{0:T(128)S(1)} copy-done((s32[5]{0:T(128)S(1)}, s32[5]{0:T(128)}, u32[]{:S(2)}) %copy-start.3) | copy-done | bytes 44
  2.6 25.5 %remap.1.slabs_ref = bf16[4,88,512]{2,1,0:T(8,128)(2,1)S(1)} custom-call(s32[5]{0:T(128)S(1)} %copy-done.3, s32[5,512]{1,0:T(8,128)S(1)} %copy-done.2, bf16[5,17,4096]{2,1,0:T(8,128)(2,1)S(1)} %copy-done.1, bf16[5,512,2048]{2,1,0:T(8,128)(2,1)} %blocks_hbm.1), custom_call_target="tpu_custom_call" | custom-call | tf_op jit(solution)/shard_map/remap/pallas_call | solution.py:229
  28.1 0.0 copy-start
  28.1 0.7 %copy-done = bf16[4,88,512]{2,1,0:T(8,128)(2,1)} copy-done((bf16[4,88,512]{2,1,0:T(8,128)(2,1)}, bf16[4,88,512]{2,1,0:T(8,128)(2,1)S(1)}, u32[]{:S(2)}) %copy-start) | copy-done | bytes 360472
  28.8 4.2 %levels.1 = bf16[5,127,512]{2,1,0:T(8,128)(2,1)} custom-call(bf16[4,88,512]{2,1,0:T(8,128)(2,1)} %copy-done, s32[127,512]{1,0:T(8,128)} %bracket_ref.1, f32[127,512]{1,0:T(8,128)} %fraction_ref.1), custom_call_target="tpu_custom_call" | custom-call | tf_op jit(solution)/shard_map/levels/pallas_call | solution.py:266
Async XLA Ops:
  0.0 1.2 %copy-start.1 = (bf16[5,17,4096]{2,1,0:T(8,128)(2,1)S(1)}, bf16[5,17,4096]{2,1,0:T(8,128)(2,1)}, u32[]{:S(2)}) copy-start(bf16[5,17,4096]{2,1,0:T(8,128)(2,1)} %source_hbm.1) | copy-start | bytes 2088964
  1.2 0.7 %copy-start.2 = (s32[5,512]{1,0:T(8,128)S(1)}, s32[5,512]{1,0:T(8,128)}, u32[]{:S(2)}) copy-start(s32[5,512]{1,0:T(8,128)} %index_ref.1) | copy-start | bytes 30724
  1.9 0.7 %copy-start.3 = (s32[5]{0:T(128)S(1)}, s32[5]{0:T(128)}, u32[]{:S(2)}) copy-start(s32[5]{0:T(128)} %inter_ref.1) | copy-start | bytes 64
  28.1 0.7 %copy-start = (bf16[4,88,512]{2,1,0:T(8,128)(2,1)}, bf16[4,88,512]{2,1,0:T(8,128)(2,1)S(1)}, u32[]{:S(2)}) copy-start(bf16[4,88,512]{2,1,0:T(8,128)(2,1)S(1)} %remap.1.slabs_ref) | copy-start | bytes 1081348

commit v2 on v1

--- a/solution.py
+++ b/solution.py
@@ -17,9 +17,9 @@
 
 def remap_kernel(
     groups, levs, depth,
-    inter_ref, index_ref, source_hbm, blocks_hbm, out_ref,
-    tile, stack32, stack, weights, request, wanted, chosen, arrived, total, slab,
-    tile_sem, weight_sem, req_send, req_recv, val_send, val_recv, lev_send, lev_recv,
+    inter_hbm, index_hbm, source_hbm, blocks_hbm, out_ref,
+    inter_ref, index_ref, tile, stack32, stack, weights, request, wanted, chosen, arrived, total, slab,
+    inter_sem, index_sem, tile_sem, weight_sem, req_send, req_recv, val_send, val_recv, lev_send, lev_recv,
 ):
     fields, slab_levels, cells = tile.shape
     rows = stack.shape[0]
@@ -39,16 +39,14 @@
             barrier, inc=1, device_id={"lev": lax.rem(my_lev + hop, levs)}, device_id_type=MESH
         )
 
+    inter_copy = pltpu.make_async_copy(inter_hbm, inter_ref, inter_sem)
+    inter_copy.start()
+    index_copy = pltpu.make_async_copy(index_hbm, index_ref, index_sem)
+    index_copy.start()
     tile_copy = pltpu.make_async_copy(source_hbm, tile, tile_sem)
     tile_copy.start()
-    weight_copies = []
-    for part in range(levs):
-        copy = pltpu.make_async_copy(
-            blocks_hbm.at[:, :, pl.ds(part * columns, columns)], weights.at[:, part], weight_sem.at[part]
-        )
-        copy.start()
-        weight_copies.append(copy)
-
+    inter_copy.wait()
+    index_copy.wait()
     slots = []
     for place in range(count):
         group = lax.rem(me + place - depth + groups, groups)
@@ -65,6 +63,13 @@
             request[place] = cells_wanted
 
     tile_copy.wait()
+    weight_copies = []
+    for part in range(levs):
+        copy = pltpu.make_async_copy(
+            blocks_hbm.at[:, :, pl.ds(part * columns, columns)], weights.at[:, part], weight_sem.at[part]
+        )
+        copy.start()
+        weight_copies.append(copy)
     for field in range(fields):
         stack32[pl.ds(field * slab_levels, slab_levels), :] = tile[field].astype(jnp.float32)
     spare = rows - fields * slab_levels
@@ -179,45 +184,62 @@
     )
 
 
-def levels_kernel(slab_levels, slabs_ref, bracket_ref, fraction_ref, out_ref, raw, table):
+def levels_kernel(slab_levels, slabs_ref, bracket_ref, fraction_ref, out_hbm, raw, table, mixed_ref, out_sem):
     levs = slabs_ref.shape[0]
-    fields, levels_out, lanes = out_ref.shape
+    strips, fields, levels_out, lanes = mixed_ref.shape
     total = levs * slab_levels
-    raw[...] = slabs_ref[...].astype(jnp.float32)
+    step = 16
+
+    def strip_copy(strip):
+        return pltpu.make_async_copy(
+            mixed_ref.at[strip],
+            out_hbm.at[:, :, pl.ds(pl.multiple_of(strip * lanes, lanes), lanes)],
+            out_sem.at[strip],
+        )
+
+    def work(strip, carry):
+        here_lanes = pl.ds(pl.multiple_of(strip * lanes, lanes), lanes)
+        raw[...] = slabs_ref[:, :, here_lanes].astype(jnp.float32)
+        for field in range(fields):
+            for lev in range(levs):
+                table[field, pl.ds(lev * slab_levels, slab_levels), :] = raw[
+                    lev, pl.ds(field * slab_levels, slab_levels), :
+                ]
+        for start in range(0, levels_out, step):
+            size = min(step, levels_out - start)
+            bracket = bracket_ref[start : start + size, here_lanes]
+            upper = fraction_ref[start : start + size, here_lanes]
+            if size < step:
+                bracket = jnp.concatenate([bracket, jnp.zeros((step - size, lanes), jnp.int32)], axis=0)
+                upper = jnp.concatenate([upper, jnp.zeros((step - size, lanes), jnp.float32)], axis=0)
+            halves = [bracket[i : i + 8] for i in range(0, step, 8)]
+            high = [half >> 3 for half in halves]
+            low = [half & 7 for half in halves]
+            below = [[jnp.zeros((8, lanes), jnp.float32) for _ in halves] for _ in range(fields)]
+            above = [[jnp.zeros((8, lanes), jnp.float32) for _ in halves] for _ in range(fields)]
+            for group in range((total - 2) // 8 + 1):
+                masks = [h == group for h in high]
+                for field in range(fields):
+                    here = table[field, pl.ds(group * 8, 8), :]
+                    over = table[field, pl.ds(group * 8 + 1, 8), :]
+                    for i, mask in enumerate(masks):
+                        below[field][i] = jnp.where(mask, rows_at(here, low[i]), below[field][i])
+                        above[field][i] = jnp.where(mask, rows_at(over, low[i]), above[field][i])
+            for field in range(fields):
+                mixed = (1.0 - upper) * jnp.concatenate(below[field], axis=0) + upper * jnp.concatenate(
+                    above[field], axis=0
+                )
+                mixed_ref[strip, field, start : start + size, :] = mixed[:size].astype(jnp.bfloat16)
+        strip_copy(strip).start()
+        return carry
+
     for field in range(fields):
-        for lev in range(levs):
-            table[field, pl.ds(lev * slab_levels, slab_levels), :] = raw[
-                lev, pl.ds(field * slab_levels, slab_levels), :
-            ]
         table[field, pl.ds(total, table.shape[1] - total), :] = jnp.zeros(
             (table.shape[1] - total, lanes), jnp.float32
         )
-    step = 16
-    for start in range(0, levels_out, step):
-        size = min(step, levels_out - start)
-        bracket = bracket_ref[start : start + size, :]
-        upper = fraction_ref[start : start + size, :]
-        if size < step:
-            bracket = jnp.concatenate([bracket, jnp.zeros((step - size, lanes), jnp.int32)], axis=0)
-            upper = jnp.concatenate([upper, jnp.zeros((step - size, lanes), jnp.float32)], axis=0)
-        halves = [bracket[i : i + 8] for i in range(0, step, 8)]
-        high = [half >> 3 for half in halves]
-        low = [half & 7 for half in halves]
-        below = [[jnp.zeros((8, lanes), jnp.float32) for _ in halves] for _ in range(fields)]
-        above = [[jnp.zeros((8, lanes), jnp.float32) for _ in halves] for _ in range(fields)]
-        for group in range((total - 2) // 8 + 1):
-            masks = [h == group for h in high]
-            for field in range(fields):
-                here = table[field, pl.ds(group * 8, 8), :]
-                over = table[field, pl.ds(group * 8 + 1, 8), :]
-                for i, mask in enumerate(masks):
-                    below[field][i] = jnp.where(mask, rows_at(here, low[i]), below[field][i])
-                    above[field][i] = jnp.where(mask, rows_at(over, low[i]), above[field][i])
-        for field in range(fields):
-            mixed = (1.0 - upper) * jnp.concatenate(below[field], axis=0) + upper * jnp.concatenate(
-                above[field], axis=0
-            )
-            out_ref[field, start : start + size, :] = mixed[:size].astype(jnp.bfloat16)
+    lax.fori_loop(0, strips, work, 0)
+    for strip in range(strips):
+        strip_copy(strip).wait()
 
 
 def local(levs, groups, source_state, intersection, index_map, blocks, bracket, fraction):
@@ -231,13 +253,15 @@
         name="remap",
         out_shape=jax.ShapeDtypeStruct((levs, rows, columns), jnp.bfloat16),
         in_specs=[
-            pl.BlockSpec(memory_space=pltpu.SMEM),
-            pl.BlockSpec(memory_space=pltpu.VMEM),
-            pl.BlockSpec(memory_space=pl.ANY),
-            pl.BlockSpec(memory_space=pl.ANY),
+            pl.BlockSpec(memory_space=pltpu.HBM),
+            pl.BlockSpec(memory_space=pltpu.HBM),
+            pl.BlockSpec(memory_space=pltpu.HBM),
+            pl.BlockSpec(memory_space=pltpu.HBM),
         ],
         out_specs=pl.BlockSpec(memory_space=pltpu.VMEM),
         scratch_shapes=[
+            pltpu.SMEM((count,), jnp.int32),
+            pltpu.VMEM((count, wide), jnp.int32),
             pltpu.VMEM((fields, slab_levels, cells), jnp.bfloat16),
             pltpu.VMEM((rows, cells), jnp.float32),
             pltpu.VMEM((rows, cells), jnp.bfloat16),
@@ -249,6 +273,8 @@
             pltpu.VMEM((levs, rows, columns), jnp.float32),
             pltpu.VMEM((levs, rows, columns), jnp.bfloat16),
             pltpu.SemaphoreType.DMA,
+            pltpu.SemaphoreType.DMA,
+            pltpu.SemaphoreType.DMA,
             pltpu.SemaphoreType.DMA((levs,)),
             pltpu.SemaphoreType.DMA((count,)),
             pltpu.SemaphoreType.DMA((count,)),
@@ -258,7 +284,12 @@
             pltpu.SemaphoreType.DMA((levs,)),
         ],
         compiler_params=pltpu.CompilerParams(
-            collective_id=0, has_side_effects=True, vmem_limit_bytes=48 * 1024 * 1024
+            collective_id=0, has_side_effects=True, vmem_limit_bytes=67043328 - 1300 * 1024
+        ),
+        cost_estimate=pl.CostEstimate(
+            flops=2 * rows * count * wide * (cells + targets),
+            bytes_accessed=2 * blocks.size + 2 * source_state.size,
+            transcendentals=0,
         ),
     )(intersection, index_map, source_state, blocks)
     levels_out, held = bracket.shape
@@ -266,18 +297,16 @@
     return pl.pallas_call(
         functools.partial(levels_kernel, slab_levels),
         name="levels",
-        grid=(held // lanes,),
         out_shape=jax.ShapeDtypeStruct((fields, levels_out, held), jnp.bfloat16),
-        in_specs=[
-            pl.BlockSpec((levs, rows, lanes), lambda i: (0, 0, i)),
-            pl.BlockSpec((levels_out, lanes), lambda i: (0, i)),
-            pl.BlockSpec((levels_out, lanes), lambda i: (0, i)),
-        ],
-        out_specs=pl.BlockSpec((fields, levels_out, lanes), lambda i: (0, 0, i)),
+        in_specs=[pl.BlockSpec(memory_space=pltpu.VMEM)] * 3,
+        out_specs=pl.BlockSpec(memory_space=pltpu.HBM),
         scratch_shapes=[
             pltpu.VMEM((levs, rows, lanes), jnp.float32),
             pltpu.VMEM((fields, round_up(levs * slab_levels, 8) + 8, lanes), jnp.float32),
+            pltpu.VMEM((held // lanes, fields, levels_out, lanes), jnp.bfloat16),
+            pltpu.SemaphoreType.DMA((held // lanes,)),
         ],
+        compiler_params=pltpu.CompilerParams(vmem_limit_bytes=8 * 1024 * 1024),
     )(slabs, bracket, fraction)
 
 

time: 33.3 us -> 29.5 us (0.89)
  local copies, waits for them, and re-layouts: 3.3 us -> 0.98 us
  Pallas kernels: 29.7 us -> 28.3 us
    unnamed x8 -> x6, local copies, waits for them, and re-layouts: 3.3 us -> 0.98 us
    pallas_call x1, Pallas kernels: 4.16 us -> 2.6 us  [local(): pl.pallas_call(functools.partial(levels_kernel, slab_levels), name='level...]
where the time goes in v2:
time: 29.5 us; the launch traced here: 29.3 us
  Pallas kernels  28.3 us (96%)
  local copies, waits for them, and re-layouts  0.98 us (3%)
    pallas_call x1, Pallas kernels, local(): pl.pallas_call(functools.partial(remap_kernel, groups, levs, depth), name...  25.7 us
    pallas_call x1, Pallas kernels, local(): pl.pallas_call(functools.partial(levels_kernel, slab_levels), name='level...  2.6 us
    unnamed x6, local copies, waits for them, and re-layouts  0.98 us

profile of v2, /device:TPU:0, one launch (start us, length us, event | category | flops | bytes accessed | tf_op | source)
XLA Modules:
  0.0 29.3 jit_solution(8001476226871457721)
XLA Ops:
  0.0 0.0 copy-start.2
  0.0 0.0 copy-start.1
  0.0 25.7 %remap.1.slabs_ref = bf16[4,88,512]{2,1,0:T(8,128)(2,1)} custom-call(s32[5]{0:T(128)} %inter_hbm.1, s32[5,512]{1,0:T(8,128)} %index_hbm.1, bf16[5,17,4096]{2,1,0:T(8,128)(2,1)} %source_hbm.1, bf16[5,512,2048]{2,1,0:T(8,128)(2,1)} %blocks_hbm.1), custom_call_target="tpu_custom_call" | custom-call | flops 2768240640 | bytes 11182080 | tf_op jit(solution)/shard_map/remap/pallas_call | solution.py:251
  25.7 0.0 copy-done.2
  25.7 0.0 copy-done.1
  25.7 0.0 copy-start
  25.7 1.0 %copy-done = bf16[4,88,512]{2,1,0:T(8,128)(2,1)S(1)} copy-done((bf16[4,88,512]{2,1,0:T(8,128)(2,1)S(1)}, bf16[4,88,512]{2,1,0:T(8,128)(2,1)}, u32[]{:S(2)}) %copy-start) | copy-done | bytes 360472
  26.7 2.6 %levels.1 = bf16[5,127,512]{2,1,0:T(8,128)(2,1)} custom-call(bf16[4,88,512]{2,1,0:T(8,128)(2,1)S(1)} %copy-done, s32[127,512]{1,0:T(8,128)S(1)} %copy-done.1, f32[127,512]{1,0:T(8,128)S(1)} %copy-done.2), custom_call_target="tpu_custom_call" | custom-call | tf_op jit(solution)/shard_map/levels/pallas_call | solution.py:297
Async XLA Ops:
  0.0 25.7 %copy-start.2 = (f32[127,512]{1,0:T(8,128)S(1)}, f32[127,512]{1,0:T(8,128)}, u32[]{:S(2)}) copy-start(f32[127,512]{1,0:T(8,128)} %fraction_ref.1) | copy-start | bytes 780292
  0.0 25.7 %copy-start.1 = (s32[127,512]{1,0:T(8,128)S(1)}, s32[127,512]{1,0:T(8,128)}, u32[]{:S(2)}) copy-start(s32[127,512]{1,0:T(8,128)} %bracket_ref.1) | copy-start | bytes 780292
  25.7 1.0 %copy-start = (bf16[4,88,512]{2,1,0:T(8,128)(2,1)S(1)}, bf16[4,88,512]{2,1,0:T(8,128)(2,1)}, u32[]{:S(2)}) copy-start(bf16[4,88,512]{2,1,0:T(8,128)(2,1)} %remap.1.slabs_ref) | copy-start | bytes 1081348

commit v3 on v2

--- a/solution.py
+++ b/solution.py
@@ -19,7 +19,7 @@
     groups, levs, depth,
     inter_hbm, index_hbm, source_hbm, blocks_hbm, out_ref,
     inter_ref, index_ref, tile, stack32, stack, weights, request, wanted, chosen, arrived, total, slab,
-    inter_sem, index_sem, tile_sem, weight_sem, req_send, req_recv, val_send, val_recv, lev_send, lev_recv,
+    inter_sem, index_sem, tile_sem, weight_sem, req_send, req_recv, val_send, val_recv, lev_send, lev_recv, own_sem,
 ):
     fields, slab_levels, cells = tile.shape
     rows = stack.shape[0]
@@ -27,6 +27,8 @@
     me = lax.axis_index("horiz")
     my_lev = lax.axis_index("lev")
     columns = out_ref.shape[2]
+    half = round_up(rows // 2, 16)
+    cuts = [(0, half), (half, rows - half)]
 
     barrier = pltpu.get_barrier_semaphore()
     offsets = [o for o in range(-depth, depth + 1) if o != 0]
@@ -89,13 +91,27 @@
             device_id_type=MESH,
         )
 
-    def value_copy(place):
+    def value_copy(place, piece):
+        first, size = cuts[piece]
         return pltpu.make_async_remote_copy(
-            src_ref=chosen.at[place],
-            dst_ref=arrived.at[2 * depth - place],
-            send_sem=val_send.at[place],
-            recv_sem=val_recv.at[2 * depth - place],
+            src_ref=chosen.at[place, pl.ds(first, size)],
+            dst_ref=arrived.at[2 * depth - place, pl.ds(first, size)],
+            send_sem=val_send.at[piece, place],
+            recv_sem=val_recv.at[piece, 2 * depth - place],
             device_id={"horiz": lax.rem(me + place - depth + groups, groups)},
+            device_id_type=MESH,
+        )
+
+    def lev_copy(hop, piece):
+        block = pl.ds(*cuts[piece])
+        if hop == 0:
+            return pltpu.make_async_copy(slab.at[0, block], out_ref.at[my_lev, block], own_sem.at[piece])
+        return pltpu.make_async_remote_copy(
+            src_ref=slab.at[hop, block],
+            dst_ref=out_ref.at[my_lev, block],
+            send_sem=lev_send.at[piece, hop],
+            recv_sem=lev_recv.at[piece, hop],
+            device_id={"lev": lax.rem(my_lev + hop, levs)},
             device_id_type=MESH,
         )
 
@@ -125,50 +141,42 @@
         place = depth + reach * (1 - 2 * (step % 2))
         request_copy(2 * depth - place).wait_recv()
         chosen[place] = select(place)
-        value_copy(place).start()
+        value_copy(place, 0).start()
         return carry
 
     lax.fori_loop(0, 2 * depth, serve, 0)
 
+    for reach in range(depth, 0, -1):
+        value_copy(depth - reach, 1).start()
+        value_copy(depth + reach, 1).start()
     for copy in weight_copies:
         copy.wait()
     order = [depth]
     for reach in range(depth, 0, -1):
         order += [depth - reach, depth + reach]
-    for number, place in enumerate(order):
-        if number:
-            value_copy(2 * depth - place).wait_recv()
-        values = arrived[place]
-        for hop in list(range(1, levs)) + [0]:
-            part = lax.rem(my_lev + hop, levs)
-            term = jnp.dot(values, weights[slots[place], part], preferred_element_type=jnp.float32)
-            if number == 0:
-                total[part] = term
-            elif number < count - 1:
-                total[part] += term
-            else:
-                done = (total[part] + term).astype(jnp.bfloat16)
-                if hop == 0:
-                    out_ref[my_lev] = done
+    for piece, (first, size) in enumerate(cuts):
+        block = pl.ds(first, size)
+        for number, place in enumerate(order):
+            if number:
+                value_copy(2 * depth - place, piece).wait_recv()
+            values = arrived[place, block]
+            for hop in list(range(1, levs)) + [0]:
+                part = lax.rem(my_lev + hop, levs)
+                term = jnp.dot(values, weights[slots[place], part], preferred_element_type=jnp.float32)
+                if number == 0:
+                    total[part, block] = term
+                elif number < count - 1:
+                    total[part, block] += term
                 else:
-                    slab[hop] = done
-                    lev_copy(hop, part, my_lev, slab, out_ref, lev_send, lev_recv).start()
-    for hop in range(1, levs):
-        lev_copy(hop, lax.rem(my_lev + hop, levs), my_lev, slab, out_ref, lev_send, lev_recv).wait()
+                    slab[hop, block] = (total[part, block] + term).astype(jnp.bfloat16)
+                    lev_copy(hop, piece).start()
+    for piece in range(len(cuts)):
+        for hop in range(levs):
+            lev_copy(hop, piece).wait()
+        for offset in offsets:
+            value_copy(depth + offset, piece).wait_send()
     for offset in offsets:
         request_copy(depth + offset).wait_send()
-        value_copy(depth + offset).wait_send()
-
-
-def lev_copy(hop, part, my_lev, slab, out_ref, lev_send, lev_recv):
-    return pltpu.make_async_remote_copy(
-        src_ref=slab.at[hop],
-        dst_ref=out_ref.at[my_lev],
-        send_sem=lev_send.at[hop],
-        recv_sem=lev_recv.at[hop],
-        device_id={"lev": part},
-        device_id_type=MESH,
-    )
 
 
 def rows_at(table, index):
@@ -184,8 +192,10 @@
     )
 
 
-def levels_kernel(slab_levels, slabs_ref, bracket_ref, fraction_ref, out_hbm, raw, table, mixed_ref, out_sem):
-    levs = slabs_ref.shape[0]
+def levels_kernel(
+    slab_levels, slabs_hbm, bracket_ref, fraction_ref, out_hbm, slabs_ref, raw, table, mixed_ref, slab_sem, out_sem
+):
+    levs = slabs_hbm.shape[0]
     strips, fields, levels_out, lanes = mixed_ref.shape
     total = levs * slab_levels
     step = 16
@@ -197,9 +207,20 @@
             out_sem.at[strip],
         )
 
+    def slab_copy(strip):
+        return pltpu.make_async_copy(
+            slabs_hbm.at[:, :, pl.ds(pl.multiple_of(strip * lanes, lanes), lanes)],
+            slabs_ref.at[strip],
+            slab_sem.at[strip],
+        )
+
+    for strip in range(strips):
+        slab_copy(strip).start()
+
     def work(strip, carry):
         here_lanes = pl.ds(pl.multiple_of(strip * lanes, lanes), lanes)
-        raw[...] = slabs_ref[:, :, here_lanes].astype(jnp.float32)
+        slab_copy(strip).wait()
+        raw[...] = slabs_ref[strip].astype(jnp.float32)
         for field in range(fields):
             for lev in range(levs):
                 table[field, pl.ds(lev * slab_levels, slab_levels), :] = raw[
@@ -258,7 +279,7 @@
             pl.BlockSpec(memory_space=pltpu.HBM),
             pl.BlockSpec(memory_space=pltpu.HBM),
         ],
-        out_specs=pl.BlockSpec(memory_space=pltpu.VMEM),
+        out_specs=pl.BlockSpec(memory_space=pltpu.HBM),
         scratch_shapes=[
             pltpu.SMEM((count,), jnp.int32),
             pltpu.VMEM((count, wide), jnp.int32),
@@ -278,10 +299,11 @@
             pltpu.SemaphoreType.DMA((levs,)),
             pltpu.SemaphoreType.DMA((count,)),
             pltpu.SemaphoreType.DMA((count,)),
-            pltpu.SemaphoreType.DMA((count,)),
-            pltpu.SemaphoreType.DMA((count,)),
-            pltpu.SemaphoreType.DMA((levs,)),
-            pltpu.SemaphoreType.DMA((levs,)),
+            pltpu.SemaphoreType.DMA((2, count)),
+            pltpu.SemaphoreType.DMA((2, count)),
+            pltpu.SemaphoreType.DMA((2, levs)),
+            pltpu.SemaphoreType.DMA((2, levs)),
+            pltpu.SemaphoreType.DMA((2,)),
         ],
         compiler_params=pltpu.CompilerParams(
             collective_id=0, has_side_effects=True, vmem_limit_bytes=67043328 - 1300 * 1024
@@ -298,15 +320,21 @@
         functools.partial(levels_kernel, slab_levels),
         name="levels",
         out_shape=jax.ShapeDtypeStruct((fields, levels_out, held), jnp.bfloat16),
-        in_specs=[pl.BlockSpec(memory_space=pltpu.VMEM)] * 3,
+        in_specs=[
+            pl.BlockSpec(memory_space=pltpu.HBM),
+            pl.BlockSpec(memory_space=pltpu.VMEM),
+            pl.BlockSpec(memory_space=pltpu.VMEM),
+        ],
         out_specs=pl.BlockSpec(memory_space=pltpu.HBM),
         scratch_shapes=[
+            pltpu.VMEM((held // lanes, levs, rows, lanes), jnp.bfloat16),
             pltpu.VMEM((levs, rows, lanes), jnp.float32),
             pltpu.VMEM((fields, round_up(levs * slab_levels, 8) + 8, lanes), jnp.float32),
             pltpu.VMEM((held // lanes, fields, levels_out, lanes), jnp.bfloat16),
             pltpu.SemaphoreType.DMA((held // lanes,)),
+            pltpu.SemaphoreType.DMA((held // lanes,)),
         ],
-        compiler_params=pltpu.CompilerParams(vmem_limit_bytes=8 * 1024 * 1024),
+        compiler_params=pltpu.CompilerParams(vmem_limit_bytes=67043328 - 700 * 1024),
     )(slabs, bracket, fraction)
 
 

time: 29.5 us -> 29.8 us (1.010)
  Pallas kernels: 28.3 us -> 29.6 us
  local copies, waits for them, and re-layouts: 0.98 us -> 0 us
    pallas_call x1, Pallas kernels: 2.6 us -> 4.55 us  [local(): pl.pallas_call(functools.partial(levels_kernel, slab_levels), name='level...]
    unnamed x6 -> x0, local copies, waits for them, and re-layouts: 0.98 us -> none
    pallas_call x1, Pallas kernels: 25.7 us -> 25.1 us  [local(): pl.pallas_call(functools.partial(remap_kernel, groups, levs, depth), name...]
where the time goes in v3:
time: 29.8 us; the launch traced here: 29.7 us
  Pallas kernels  29.6 us (99%)
    pallas_call x1, Pallas kernels, local(): pl.pallas_call(functools.partial(remap_kernel, groups, levs, depth), name...  25.1 us
    pallas_call x1, Pallas kernels, local(): pl.pallas_call(functools.partial(levels_kernel, slab_levels), name='level...  4.55 us

profile of v3, /device:TPU:0, one launch (start us, length us, event | category | flops | bytes accessed | tf_op | source)
XLA Modules:
  0.0 29.7 jit_solution(16363471890815113872)
XLA Ops:
  0.0 25.1 %remap.1.slabs_hbm = bf16[4,88,512]{2,1,0:T(8,128)(2,1)} custom-call(s32[5]{0:T(128)} %inter_hbm.1, s32[5,512]{1,0:T(8,128)} %index_hbm.1, bf16[5,17,4096]{2,1,0:T(8,128)(2,1)} %source_hbm.1, bf16[5,512,2048]{2,1,0:T(8,128)(2,1)} %blocks_hbm.1), custom_call_target="tpu_custom_call" | custom-call | flops 2768240640 | bytes 11182080 | tf_op jit(solution)/shard_map/remap/pallas_call | solution.py:272
  25.1 4.6 %levels.1 = bf16[5,127,512]{2,1,0:T(8,128)(2,1)} custom-call(bf16[4,88,512]{2,1,0:T(8,128)(2,1)} %remap.1.slabs_hbm, s32[127,512]{1,0:T(8,128)} %bracket_ref.1, f32[127,512]{1,0:T(8,128)} %fraction_ref.1), custom_call_target="tpu_custom_call" | custom-call | tf_op jit(solution)/shard_map/levels/pallas_call | solution.py:319

commit v4 on v3

--- a/solution.py
+++ b/solution.py
@@ -193,7 +193,8 @@
 
 
 def levels_kernel(
-    slab_levels, slabs_hbm, bracket_ref, fraction_ref, out_hbm, slabs_ref, raw, table, mixed_ref, slab_sem, out_sem
+    slab_levels, slabs_hbm, bracket_hbm, fraction_hbm, out_hbm,
+    slabs_ref, brackets, fractions, raw, table, mixed_ref, slab_sem, bracket_sem, fraction_sem, out_sem,
 ):
     levs = slabs_hbm.shape[0]
     strips, fields, levels_out, lanes = mixed_ref.shape
@@ -214,12 +215,29 @@
             slab_sem.at[strip],
         )
 
+    def bracket_copy(strip):
+        return pltpu.make_async_copy(
+            bracket_hbm.at[:, pl.ds(pl.multiple_of(strip * lanes, lanes), lanes)],
+            brackets.at[strip],
+            bracket_sem.at[strip],
+        )
+
+    def fraction_copy(strip):
+        return pltpu.make_async_copy(
+            fraction_hbm.at[:, pl.ds(pl.multiple_of(strip * lanes, lanes), lanes)],
+            fractions.at[strip],
+            fraction_sem.at[strip],
+        )
+
     for strip in range(strips):
         slab_copy(strip).start()
+        bracket_copy(strip).start()
+        fraction_copy(strip).start()
 
     def work(strip, carry):
-        here_lanes = pl.ds(pl.multiple_of(strip * lanes, lanes), lanes)
         slab_copy(strip).wait()
+        bracket_copy(strip).wait()
+        fraction_copy(strip).wait()
         raw[...] = slabs_ref[strip].astype(jnp.float32)
         for field in range(fields):
             for lev in range(levs):
@@ -228,8 +246,8 @@
                 ]
         for start in range(0, levels_out, step):
             size = min(step, levels_out - start)
-            bracket = bracket_ref[start : start + size, here_lanes]
-            upper = fraction_ref[start : start + size, here_lanes]
+            bracket = brackets[strip, start : start + size, :]
+            upper = fractions[strip, start : start + size, :]
             if size < step:
                 bracket = jnp.concatenate([bracket, jnp.zeros((step - size, lanes), jnp.int32)], axis=0)
                 upper = jnp.concatenate([upper, jnp.zeros((step - size, lanes), jnp.float32)], axis=0)
@@ -320,17 +338,17 @@
         functools.partial(levels_kernel, slab_levels),
         name="levels",
         out_shape=jax.ShapeDtypeStruct((fields, levels_out, held), jnp.bfloat16),
-        in_specs=[
-            pl.BlockSpec(memory_space=pltpu.HBM),
-            pl.BlockSpec(memory_space=pltpu.VMEM),
-            pl.BlockSpec(memory_space=pltpu.VMEM),
-        ],
+        in_specs=[pl.BlockSpec(memory_space=pltpu.HBM)] * 3,
         out_specs=pl.BlockSpec(memory_space=pltpu.HBM),
         scratch_shapes=[
             pltpu.VMEM((held // lanes, levs, rows, lanes), jnp.bfloat16),
+            pltpu.VMEM((held // lanes, levels_out, lanes), jnp.int32),
+            pltpu.VMEM((held // lanes, levels_out, lanes), jnp.float32),
             pltpu.VMEM((levs, rows, lanes), jnp.float32),
             pltpu.VMEM((fields, round_up(levs * slab_levels, 8) + 8, lanes), jnp.float32),
             pltpu.VMEM((held // lanes, fields, levels_out, lanes), jnp.bfloat16),
+            pltpu.SemaphoreType.DMA((held // lanes,)),
+            pltpu.SemaphoreType.DMA((held // lanes,)),
             pltpu.SemaphoreType.DMA((held // lanes,)),
             pltpu.SemaphoreType.DMA((held // lanes,)),
         ],

time: 29.8 us -> 29.1 us (0.977)
  Pallas kernels: 29.6 us -> 28.9 us
    pallas_call x1, Pallas kernels: 4.55 us -> 3.8 us  [local(): pl.pallas_call(functools.partial(levels_kernel, slab_levels), name='level...]
where the time goes in v4:
time: 29.1 us; the launch traced here: 28.9 us
  Pallas kernels  28.9 us (99%)
    pallas_call x1, Pallas kernels, local(): pl.pallas_call(functools.partial(remap_kernel, groups, levs, depth), name...  25.1 us
    pallas_call x1, Pallas kernels, local(): pl.pallas_call(functools.partial(levels_kernel, slab_levels), name='level...  3.8 us

profile of v4, /device:TPU:0, one launch (start us, length us, event | category | flops | bytes accessed | tf_op | source)
XLA Modules:
  0.0 28.9 jit_solution(12735060323866265517)
XLA Ops:
  0.0 25.1 %remap.1.slabs_hbm = bf16[4,88,512]{2,1,0:T(8,128)(2,1)} custom-call(s32[5]{0:T(128)} %inter_hbm.1, s32[5,512]{1,0:T(8,128)} %index_hbm.1, bf16[5,17,4096]{2,1,0:T(8,128)(2,1)} %source_hbm.1, bf16[5,512,2048]{2,1,0:T(8,128)(2,1)} %blocks_hbm.1), custom_call_target="tpu_custom_call" | custom-call | flops 2768240640 | bytes 11182080 | tf_op jit(solution)/shard_map/remap/pallas_call | solution.py:290
  25.1 3.8 %levels.1 = bf16[5,127,512]{2,1,0:T(8,128)(2,1)} custom-call(bf16[4,88,512]{2,1,0:T(8,128)(2,1)} %remap.1.slabs_hbm, s32[127,512]{1,0:T(8,128)} %bracket_hbm.1, f32[127,512]{1,0:T(8,128)} %fraction_hbm.1), custom_call_target="tpu_custom_call" | custom-call | tf_op jit(solution)/shard_map/levels/pallas_call | solution.py:337
